TPU v7x, 32 devices: a whole 2x2x4 slice. The times are simulated.
32 devices in a mesh: seq: 8 (over z, x), head: 4 (over y, core).
Axes of the slice: x: 2, y: 2, z: 4, core: 2. Of those that a mesh axis runs over, the one named last changes fastest.
Arguments:
- q_latent: bfloat16 [2048, 1536], P('seq', 'head'), may hold values from -6 to 6
- kv_latent: bfloat16 [2048, 512], P('seq', 'head'), may hold values from -6 to 6
- k_rope: bfloat16 [2048, 64], P('seq'), may hold values from -6 to 6
- segment_ids: int32 [2048], P('seq'), may hold values from 0 to 7, as said below
- w_q_nope: bfloat16 [1536, 16384], P('seq', 'head'), may hold values from -6 to 6
- w_q_rope: bfloat16 [1536, 8192], P('seq', 'head'), may hold values from -6 to 6
- w_kv_nope: bfloat16 [512, 16384], P('seq', 'head'), may hold values from -6 to 6
- threshold: float32 [1], replicated, may hold values from 3.5 to 5.5
Outputs:
- new_q_nope: bfloat16 [1536, 16384], P('seq', 'head')
- new_q_rope: bfloat16 [1536, 8192], P('seq', 'head')
- new_kv_nope: bfloat16 [512, 16384], P('seq', 'head')
- head_max: float32 [128], P('head')
- row_max: float32 [2048, 128], P('seq', 'head')
Inputs may be any that keep to these rules, and one draw needn't show every extreme that they name: segment_ids never fall along the tokens and each document has 1 to 768 tokens.
All inputs are finite; a program needn't handle non-finite values.
Results may differ from a plain program's by a relative error of at most 0.0034.
Values may be sent and summed in bfloat16 or wider, within the bound.
A program may use at most 128 MiB of HBM per device.

v0:
```python
import math
import jax
import jax.numpy as jnp
from jax import lax
from jax.sharding import PartitionSpec as P

D_NOPE = 128
D_ROPE = 64
QLORA = 1536
KVLORA = 512
REACH = 3


def as_sent(value):
    return jax.tree.map(lambda a: a.astype(jnp.bfloat16) if a.dtype == jnp.float32 else a, value)


def from_partner(value, axis, stride):
    mask = 2**stride
    pairs = [(source, source ^ mask) for source in range(lax.axis_size(axis))]
    return lax.ppermute(value, axis, pairs)


def shifted(block, axis, distance):
    devices = range(lax.axis_size(axis))
    route = [(i - distance, i) for i in devices if i - distance in devices]
    return lax.ppermute(block, axis, route)


def score_max(query_nope, query_rope, key_nope, key_rope, allowed):
    nope = jnp.einsum("qhd,khd->hqk", query_nope, key_nope, preferred_element_type=jnp.float32)
    rope = jnp.einsum("qhd,kd->hqk", query_rope, key_rope, preferred_element_type=jnp.float32)
    scores = (nope + rope) * (1.0 / math.sqrt(D_NOPE + D_ROPE))
    return jnp.max(jnp.where(allowed[None], scores, jnp.float32(-1e30)), axis=2)


def masked_max(compute, operands):
    return compute(*operands)


def spread_columns(weight, width, quarter, copies):
    pieces = weight.reshape(weight.shape[0], 4, quarter * width).transpose(1, 0, 2)
    return jnp.tile(pieces, (copies, 1, 1))


def body(q_latent, kv_latent, k_rope, segment_ids, w_q_nope, w_q_rope, w_kv_nope, threshold):
    q_whole, kv_whole = (
        lax.all_gather(q_latent, "head", axis=1, tiled=True),
        lax.all_gather(kv_latent, "head", axis=1, tiled=True),
    )
    rows = q_whole.shape[0]
    heads = w_q_nope.shape[1] // D_NOPE
    q_scale = 1.0 / math.sqrt(QLORA)
    k_scale = 1.0 / math.sqrt(KVLORA)
    place = lax.axis_index("seq")
    quarter = heads // 4
    copies = lax.axis_size("seq") // 4
    slot = place % 4
    sent = (
        spread_columns(w_q_nope, D_NOPE, quarter, copies),
        spread_columns(w_q_rope, D_ROPE, quarter, copies),
        spread_columns(w_kv_nope, D_NOPE, quarter, copies),
    )
    got_nope, got_rope, got_kv = (
        lax.all_to_all(sent[0], "seq", split_axis=0, concat_axis=1, tiled=True),
        lax.all_to_all(sent[1], "seq", split_axis=0, concat_axis=1, tiled=True),
        lax.all_to_all(sent[2], "seq", split_axis=0, concat_axis=1, tiled=True),
    )
    sub_nope = got_nope.reshape(QLORA, quarter * D_NOPE)
    sub_rope = got_rope.reshape(QLORA, quarter * D_ROPE)
    sub_kv = got_kv.reshape(KVLORA, quarter * D_NOPE)
    group = (q_whole, kv_whole, k_rope)
    for level in range(2):
        partner = jax.tree.map(
            lambda part, own: part.astype(own.dtype),
            from_partner(as_sent(group), "seq", level),
            group,
        )
        upper = place // (1 << level) % 2 == 1
        group = tuple(
            (
                jnp.where(
                    upper, jnp.concatenate([other, mine], 0), jnp.concatenate([mine, other], 0)
                )
                for mine, other in zip(group, partner)
            )
        )
    group_q, group_kv, group_rope = group
    early_kv, early_rope = shifted(
        (group_kv[(4 - REACH) * rows :], group_rope[(4 - REACH) * rows :]), "seq", 4
    )
    keys_kv = jnp.concatenate([early_kv, group_kv], 0)
    keys_rope = jnp.concatenate([early_rope, group_rope], 0)
    key_nope = (
        (jnp.dot(keys_kv, sub_kv, preferred_element_type=jnp.float32) * k_scale)
        .astype(jnp.bfloat16)
        .reshape(keys_kv.shape[0], quarter, D_NOPE)
    )
    query_nope = (
        (jnp.dot(group_q, sub_nope, preferred_element_type=jnp.float32) * q_scale)
        .astype(jnp.bfloat16)
        .reshape(4 * rows, quarter, D_NOPE)
    )
    query_rope = (
        (jnp.dot(group_q, sub_rope, preferred_element_type=jnp.float32) * q_scale)
        .astype(jnp.bfloat16)
        .reshape(4 * rows, quarter, D_ROPE)
    )
    all_segs = lax.all_gather(segment_ids, "seq", axis=0, tiled=True)
    padded_segs = jnp.concatenate([jnp.full((REACH * rows,), -1, jnp.int32), all_segs], 0)
    first = place // 4 * 4
    window = (REACH + 1) * rows
    block_rows = []
    for local in range(4):
        block = first + local
        query_seg = lax.dynamic_slice_in_dim(all_segs, block * rows, rows, 0)
        key_seg = lax.dynamic_slice_in_dim(padded_segs, block * rows, window, 0)
        query_pos = block * rows + jnp.arange(rows, dtype=jnp.int32)
        key_pos = (block - REACH) * rows + jnp.arange(window, dtype=jnp.int32)
        allowed = (
            (query_seg[:, None] == key_seg[None, :])
            & (key_pos[None, :] <= query_pos[:, None])
            & (key_pos[None, :] >= 0)
        )
        operands = (
            query_nope[local * rows : (local + 1) * rows],
            query_rope[local * rows : (local + 1) * rows],
            key_nope[local * rows : local * rows + window],
            keys_rope[local * rows : local * rows + window],
            allowed,
        )
        block_rows.append(masked_max(score_max, operands))
    stacked = jnp.stack(block_rows, 0)[None]
    for level in range(2):
        partner = from_partner(stacked, "seq", level)
        upper = place // (1 << level) % 2 == 1
        stacked = jnp.where(
            upper, jnp.concatenate([partner, stacked], 0), jnp.concatenate([stacked, partner], 0)
        )
    own = lax.dynamic_index_in_dim(stacked, slot, 1, False)
    row_max = own.reshape(heads, rows).T
    local_heads = jnp.max(row_max, axis=0)
    head_max = lax.pmax(local_heads, "seq")
    clip = threshold[0] / jnp.maximum(head_max, threshold[0])
    root = jnp.sqrt(clip)
    new_q_nope = (w_q_nope.astype(jnp.float32) * jnp.repeat(root, D_NOPE)[None, :]).astype(
        jnp.bfloat16
    )
    new_q_rope = (w_q_rope.astype(jnp.float32) * jnp.repeat(clip, D_ROPE)[None, :]).astype(
        jnp.bfloat16
    )
    new_kv_nope = (w_kv_nope.astype(jnp.float32) * jnp.repeat(root, D_NOPE)[None, :]).astype(
        jnp.bfloat16
    )
    return (new_q_nope, new_q_rope, new_kv_nope, head_max, row_max)


def solution(mesh):
    in_specs = (
        P("seq", "head"),
        P("seq", "head"),
        P("seq", None),
        P("seq"),
        P("seq", "head"),
        P("seq", "head"),
        P("seq", "head"),
        P(),
    )
    out_specs = (P("seq", "head"), P("seq", "head"), P("seq", "head"), P("head"), P("seq", "head"))
    return jax.shard_map(body, mesh=mesh, in_specs=in_specs, out_specs=out_specs, check_vma=False)
```

profile of v0, /device:TPU:0, one launch (start us, length us, event | category | flops | bytes accessed | tf_op | source)
XLA Modules:
  0.0 299.3 jit_solution(7385676597361516628)
XLA Ops:
  3.4 7.3 %all-to-all-start.1 = ((bf16[8,64,1024]{2,1,0:T(8,128)(2,1)}), bf16[8,64,1024]{2,1,0:T(8,128)(2,1)S(1)}, u32[]{:S(2)}, u32[]{:S(2)}) async-start(bf16[8,64,1024]{2,1,0:T(8,128)(2,1)} %bitcast.8), calls=%async_computation.1 | async-start | bytes 2097152 | tf_op jit(solution)/shard_map/all_to_all | solution.py:67
  11.4 25.0 %all-to-all-done.1 = bf16[8,64,1024]{2,1,0:T(8,128)(2,1)S(1)} async-done(((bf16[8,64,1024]{2,1,0:T(8,128)(2,1)}), bf16[8,64,1024]{2,1,0:T(8,128)(2,1)S(1)}, u32[]{:S(2)}, u32[]{:S(2)}) %all-to-all-start.1) | async-done | bytes 1048608 | tf_op jit(solution)/shard_map/all_to_all | solution.py:67
  37.9 4.3 %all-to-all-start.2 = ((bf16[8,192,512]{2,1,0:T(8,128)(2,1)}), bf16[8,192,512]{2,1,0:T(8,128)(2,1)}, u32[]{:S(2)}, u32[]{:S(2)}) async-start(bf16[8,192,512]{2,1,0:T(8,128)(2,1)} %bitcast.13), calls=%async_computation.2 | async-start | bytes 3145728 | tf_op jit(solution)/shard_map/all_to_all | solution.py:66
  43.9 34.9 %all-to-all-done.2 = bf16[8,192,512]{2,1,0:T(8,128)(2,1)} async-done(((bf16[8,192,512]{2,1,0:T(8,128)(2,1)}), bf16[8,192,512]{2,1,0:T(8,128)(2,1)}, u32[]{:S(2)}, u32[]{:S(2)}) %all-to-all-start.2) | async-done | bytes 1572896 | tf_op jit(solution)/shard_map/all_to_all | solution.py:66
  78.8 2.1 tile.12
  81.0 4.6 %all-to-all-start = ((bf16[8,192,1024]{2,1,0:T(8,128)(2,1)}), bf16[8,192,1024]{2,1,0:T(8,128)(2,1)}, u32[]{:S(2)}, u32[]{:S(2)}) async-start(bf16[8,192,1024]{2,1,0:T(8,128)(2,1)} %bitcast.4), calls=%async_computation | async-start | bytes 6291456 | tf_op jit(solution)/shard_map/all_to_all | solution.py:65
  87.5 5.8 %all_gather.11 = bf16[256,512]{1,0:T(8,128)(2,1)S(1)} all-gather(bf16[256,128]{1,0:T(8,128)(2,1)S(1)} %copy-done.15), channel_id=1, replica_groups=mesh['seq'=8,'head'=4] {'head'}, dimensions={1}, use_global_device_ids=true | all-gather | bytes 327680 | tf_op jit(solution)/shard_map/all_gather | solution.py:49
  93.5 8.6 %all_gather.10 = bf16[256,1536]{1,0:T(8,128)(2,1)S(1)} all-gather(bf16[256,384]{1,0:T(8,128)(2,1)S(1)} %copy-done.14), channel_id=1, replica_groups=mesh['seq'=8,'head'=4] {'head'}, dimensions={1}, use_global_device_ids=true | all-gather | bytes 983040 | tf_op jit(solution)/shard_map/all_gather | solution.py:48
  104.0 50.2 %all-gather = s32[8,1,256]{2,1,0:T(1,128)S(1)} all-gather(s32[1,1,256]{2,1,0:T(1,128)S(1)} %bitcast.118), channel_id=1, replica_groups=mesh['seq'=8,'head'=4] {'seq'}, dimensions={0}, use_global_device_ids=true | all-gather | bytes 9216 | tf_op jit(solution)/shard_map/all_gather | solution.py:109
  154.6 11.1 %collective-permute-start.3 = (bf16[512,512]{1,0:T(8,128)(2,1)S(1)}, bf16[512,512]{1,0:T(8,128)(2,1)S(1)}, u32[]{:S(2)}, u32[]{:S(2)}) collective-permute-start(bf16[512,512]{1,0:T(8,128)(2,1)S(1)} %maximum_select_fusion.5), channel_id=1, source_target_pairs={{0,8},{4,12},{8,0},{12,4},{16,24},{20,28},{24,16},{28,20},{1,9},{5... | collective-permute-start | bytes 1572872 | tf_op jit(solution)/shard_map/ppermute | solution.py:21
  167.3 6.2 %collective-permute-done.3 = bf16[512,512]{1,0:T(8,128)(2,1)S(1)} collective-permute-done((bf16[512,512]{1,0:T(8,128)(2,1)S(1)}, bf16[512,512]{1,0:T(8,128)(2,1)S(1)}, u32[]{:S(2)}, u32[]{:S(2)}) %collective-permute-start.3) | collective-permute-done | bytes 524320 | tf_op jit(solution)/shard_map/ppermute | solution.py:21
  174.1 4.7 %collective-permute-start.4 = (bf16[768,512]{1,0:T(8,128)(2,1)S(1)}, bf16[768,512]{1,0:T(8,128)(2,1)S(1)}, u32[]{:S(2)}, u32[]{:S(2)}) collective-permute-start(bf16[768,512]{1,0:T(8,128)(2,1)S(1)} %slice.117), channel_id=1, source_target_pairs={{0,16},{4,20},{8,24},{12,28},{1,17},{5,21},{9,25},{13,29},{2,18},{... | collective-permute-start | bytes 2359304 | tf_op jit(solution)/shard_map/ppermute | solution.py:27
  182.0 44.8 %collective-permute-done.6 = bf16[512,64]{0,1:T(8,128)(2,1)S(1)} collective-permute-done((bf16[512,64]{0,1:T(8,128)(2,1)S(1)}, bf16[512,64]{0,1:T(8,128)(2,1)S(1)}, u32[]{:S(2)}, u32[]{:S(2)}) %collective-permute-start.6) | collective-permute-done | bytes 65568 | tf_op jit(solution)/shard_map/ppermute | solution.py:21
  227.4 2.1 collective-permute-start.7
  229.6 2.2 multiply_convert_fusion
  231.8 3.0 fusion.37
  234.7 3.9 %multiply_convert_fusion.3 = bf16[1024,512]{0,1:T(8,128)(2,1)S(1)} fusion(bf16[1536,512]{1,0:T(8,128)(2,1)} %bitcast.14, bf16[512,1536]{1,0:T(8,128)(2,1)S(1)} %maximum_select_fusion.1, bf16[512,1536]{1,0:T(8,128)(2,1)S(1)} %collective-permute-done.1, pred[]{:T(512)S(6)} %eq.82), kind=kOutput, calls=%fused_computation.20 | convolution fusion | flops 1625817088 | bytes 5767169 | tf_op jit(solution)/shard_map/dot_general | solution.py:105
  239.5 7.3 %multiply_convert_fusion.1 = bf16[1024,1024]{0,1:T(8,128)(2,1)S(1)} fusion(bf16[1536,1024]{1,0:T(8,128)(2,1)} %bitcast.5, bf16[512,1536]{1,0:T(8,128)(2,1)} %copy-done.8, bf16[512,1536]{1,0:T(8,128)(2,1)} %copy-done.19, pred[]{:T(512)S(6)} %eq.82), kind=kOutput, calls=%fused_computation.17 | convolution fusion | flops 3237478400 | bytes 8388609 | tf_op jit(solution)/shard_map/dot_general | solution.py:100
  256.5 3.0 %fusion.11 = f32[8,256]{1,0:T(8,128)S(1)} fusion(f32[8,256,1024]{2,1,0:T(8,128)S(1)} %fusion.41, pred[256,1024]{1,0:T(8,128)(4,1)S(1)} %and_and_fusion.3, bf16[256,8,64]{0,2,1:T(8,128)(2,1)S(1)} %bitcast.109, bf16[1024,64]{0,1:T(8,128)(2,1)S(1)} %maximum_select_fusion.6, bf16[768,64]{0,1:T(8,128)(2,1)} %collective-permute-done.7), kind=kOutput, calls=%fused_computation.15 | convolution fusion | flops 277084160 | bytes 9150464 | tf_op jit(solution)/shard_map/qhd,kd->hqk/dot_general | solution.py:32
  259.6 2.9 fusion.5
  262.5 3.1 %fusion.8 = f32[8,256]{1,0:T(8,128)S(1)} fusion(f32[8,256,1024]{2,1,0:T(8,128)S(1)} %fusion.42, pred[256,1024]{1,0:T(8,128)(4,1)S(1)} %get-tuple-element.30, bf16[256,8,64]{0,2,1:T(8,128)(2,1)S(1)} %bitcast.107, bf16[1024,64]{0,1:T(8,128)(2,1)S(1)} %maximum_select_fusion.6, bf16[768,64]{0,1:T(8,128)(2,1)} %collective-permute-done.7), kind=kOutput, calls=%fused_computation.11 | convolution fusion | flops 277084160 | bytes 9150464 | tf_op jit(solution)/shard_map/qhd,kd->hqk/dot_general | solution.py:32
  265.7 3.4 %collective-permute-start.8 = (f32[1,4,8,256]{3,2,0,1:T(8,128)S(1)}, f32[1,4,8,256]{3,2,0,1:T(8,128)S(1)}, u32[]{:S(2)}, u32[]{:S(2)}) collective-permute-start(f32[1,4,8,256]{3,2,0,1:T(8,128)S(1)} %maximum_bitcast_fusion), channel_id=1, source_target_pairs={{0,4},{4,0},{8,12},{12,8},{16,20},{20,16},{24,28},{28,24},{1,5},{5... | collective-permute-start | bytes 98312 | tf_op jit(solution)/shard_map/ppermute | solution.py:21
  271.0 2.5 collective-permute-start.9
  276.5 19.1 %pmax.7 = f32[32]{0:T(128)S(1)} all-reduce(f32[32]{0:T(128)S(1)} %reduce_max.52), channel_id=1, replica_groups=mesh['seq'=8,'head'=4] {'seq'}, use_global_device_ids=true, to_apply=%region_5.6 | all-reduce | flops 32 | bytes 256 | tf_op jit(solution)/shard_map/pmax | solution.py:143
  (104 shorter events, 35.2 us)
Async XLA Ops:
  0.6 10.1 %copy-start.5 = (bf16[192,2048]{1,0:T(8,128)(2,1)S(1)}, bf16[192,2048]{1,0:T(8,128)(2,1)}, u32[]{:S(2)}) copy-start(bf16[192,2048]{1,0:T(8,128)(2,1)} %param.13) | copy-start | bytes 2359300
  3.4 33.0 %all-to-all-start.1 = ((bf16[8,64,1024]{2,1,0:T(8,128)(2,1)}), bf16[8,64,1024]{2,1,0:T(8,128)(2,1)S(1)}, u32[]{:S(2)}, u32[]{:S(2)}) async-start(bf16[8,64,1024]{2,1,0:T(8,128)(2,1)} %bitcast.8), calls=%async_computation.1 | async-start | bytes 2097152 | tf_op jit(solution)/shard_map/all_to_all | solution.py:67
  11.4 30.8 %copy-start.3 = (bf16[192,4096]{1,0:T(8,128)(2,1)S(1)}, bf16[192,4096]{1,0:T(8,128)(2,1)}, u32[]{:S(2)}) copy-start(bf16[192,4096]{1,0:T(8,128)(2,1)} %param.12) | copy-start | bytes 4718596
  37.9 40.9 %all-to-all-start.2 = ((bf16[8,192,512]{2,1,0:T(8,128)(2,1)}), bf16[8,192,512]{2,1,0:T(8,128)(2,1)}, u32[]{:S(2)}, u32[]{:S(2)}) async-start(bf16[8,192,512]{2,1,0:T(8,128)(2,1)} %bitcast.13), calls=%async_computation.2 | async-start | bytes 3145728 | tf_op jit(solution)/shard_map/all_to_all | solution.py:66
  80.9 4.6 %copy-start.16 = (bf16[256,64]{0,1:T(8,128)(2,1)S(1)}, bf16[256,64]{0,1:T(8,128)(2,1)}, u32[]{:S(2)}) copy-start(bf16[256,64]{0,1:T(8,128)(2,1)} %param.10) | copy-start | bytes 98308
  80.9 6.5 %copy-start.15 = (bf16[256,128]{1,0:T(8,128)(2,1)S(1)}, bf16[256,128]{1,0:T(8,128)(2,1)}, u32[]{:S(2)}) copy-start(bf16[256,128]{1,0:T(8,128)(2,1)} %param.9) | copy-start | bytes 196612
  80.9 12.5 %copy-start.14 = (bf16[256,384]{1,0:T(8,128)(2,1)S(1)}, bf16[256,384]{1,0:T(8,128)(2,1)}, u32[]{:S(2)}) copy-start(bf16[256,384]{1,0:T(8,128)(2,1)} %param.8) | copy-start | bytes 589828
  81.0 23.1 %copy-start.17 = (s32[256]{0:T(256)S(1)}, s32[256]{0:T(256)}, u32[]{:S(2)}) copy-start(s32[256]{0:T(256)} %param.11) | copy-start | bytes 3076
  81.0 158.5 %all-to-all-start = ((bf16[8,192,1024]{2,1,0:T(8,128)(2,1)}), bf16[8,192,1024]{2,1,0:T(8,128)(2,1)}, u32[]{:S(2)}, u32[]{:S(2)}) async-start(bf16[8,192,1024]{2,1,0:T(8,128)(2,1)} %bitcast.4), calls=%async_computation | async-start | bytes 6291456 | tf_op jit(solution)/shard_map/all_to_all | solution.py:65
  85.6 94.5 %collective-permute-start.5 = (bf16[256,64]{0,1:T(8,128)(2,1)S(1)}, bf16[256,64]{0,1:T(8,128)(2,1)S(1)}, u32[]{:S(2)}, u32[]{:S(2)}) collective-permute-start(bf16[256,64]{0,1:T(8,128)(2,1)S(1)} %copy-done.16), channel_id=1, source_target_pairs={{0,4},{4,0},{8,12},{12,8},{16,20},{20,16},{24,28},{28,24},{1,5},{5... | collective-permute-start | bytes 98312 | tf_op jit(solution)/shard_map/ppermute | solution.py:21
  93.3 61.1 %collective-permute-start.2 = (bf16[256,512]{1,0:T(8,128)(2,1)S(1)}, bf16[256,512]{1,0:T(8,128)(2,1)S(1)}, u32[]{:S(2)}, u32[]{:S(2)}) collective-permute-start(bf16[256,512]{1,0:T(8,128)(2,1)S(1)} %all_gather.11), channel_id=1, source_target_pairs={{0,4},{4,0},{8,12},{12,8},{16,20},{20,16},{24,28},{28,24},{1,5},{5... | collective-permute-start | bytes 786440 | tf_op jit(solution)/shard_map/ppermute | solution.py:21
  102.1 76.7 %collective-permute-start = (bf16[256,1536]{1,0:T(8,128)(2,1)S(1)}, bf16[256,1536]{1,0:T(8,128)(2,1)S(1)}, u32[]{:S(2)}, u32[]{:S(2)}) collective-permute-start(bf16[256,1536]{1,0:T(8,128)(2,1)S(1)} %all_gather.10), channel_id=1, source_target_pairs={{0,4},{4,0},{8,12},{12,8},{16,20},{20,16},{24,28},{28,24},{1,5},{5... | collective-permute-start | bytes 2359304 | tf_op jit(solution)/shard_map/ppermute | solution.py:21
  154.6 18.9 %collective-permute-start.3 = (bf16[512,512]{1,0:T(8,128)(2,1)S(1)}, bf16[512,512]{1,0:T(8,128)(2,1)S(1)}, u32[]{:S(2)}, u32[]{:S(2)}) collective-permute-start(bf16[512,512]{1,0:T(8,128)(2,1)S(1)} %maximum_select_fusion.5), channel_id=1, source_target_pairs={{0,8},{4,12},{8,0},{12,4},{16,24},{20,28},{24,16},{28,20},{1,9},{5... | collective-permute-start | bytes 1572872 | tf_op jit(solution)/shard_map/ppermute | solution.py:21
  174.0 55.6 %copy-start.10 = (bf16[8,64,1024]{2,1,0:T(8,128)(2,1)S(1)}, bf16[8,64,1024]{2,1,0:T(8,128)(2,1)}, u32[]{:S(2)}) copy-start(bf16[8,64,1024]{2,1,0:T(8,128)(2,1)} %copy-done.9) | copy-start | bytes 3145732
  174.1 55.5 %collective-permute-start.4 = (bf16[768,512]{1,0:T(8,128)(2,1)S(1)}, bf16[768,512]{1,0:T(8,128)(2,1)S(1)}, u32[]{:S(2)}, u32[]{:S(2)}) collective-permute-start(bf16[768,512]{1,0:T(8,128)(2,1)S(1)} %slice.117), channel_id=1, source_target_pairs={{0,16},{4,20},{8,24},{12,28},{1,17},{5,21},{9,25},{13,29},{2,18},{... | collective-permute-start | bytes 2359304 | tf_op jit(solution)/shard_map/ppermute | solution.py:27
  179.4 55.3 %copy-start.8 = (bf16[512,1536]{1,0:T(8,128)(2,1)}, bf16[512,1536]{1,0:T(8,128)(2,1)S(1)}, u32[]{:S(2)}) copy-start(bf16[512,1536]{1,0:T(8,128)(2,1)S(1)} %maximum_select_fusion.1) | copy-start | bytes 4718596
  179.4 55.3 %collective-permute-start.1 = (bf16[512,1536]{1,0:T(8,128)(2,1)S(1)}, bf16[512,1536]{1,0:T(8,128)(2,1)S(1)}, u32[]{:S(2)}, u32[]{:S(2)}) collective-permute-start(bf16[512,1536]{1,0:T(8,128)(2,1)S(1)} %maximum_select_fusion.1), channel_id=1, source_target_pairs={{0,8},{4,12},{8,0},{12,4},{16,24},{20,28},{24,16},{28,20},{1,9},{5... | collective-permute-start | bytes 4718600 | tf_op jit(solution)/shard_map/ppermute | solution.py:21
  180.1 46.6 %collective-permute-start.6 = (bf16[512,64]{0,1:T(8,128)(2,1)S(1)}, bf16[512,64]{0,1:T(8,128)(2,1)S(1)}, u32[]{:S(2)}, u32[]{:S(2)}) collective-permute-start(bf16[512,64]{0,1:T(8,128)(2,1)S(1)} %maximum_select_fusion.7), channel_id=1, source_target_pairs={{0,8},{4,12},{8,0},{12,4},{16,24},{20,28},{24,16},{28,20},{1,9},{5... | collective-permute-start | bytes 196616 | tf_op jit(solution)/shard_map/ppermute | solution.py:21
  227.4 29.1 %collective-permute-start.7 = (bf16[768,64]{0,1:T(8,128)(2,1)}, bf16[768,64]{0,1:T(8,128)(2,1)}, u32[]{:S(2)}, u32[]{:S(2)}) collective-permute-start(bf16[768,64]{0,1:T(8,128)(2,1)} %slice.119), channel_id=1, source_target_pairs={{0,16},{4,20},{8,24},{12,28},{1,17},{5,21},{9,25},{13,29},{2,18},{... | collective-permute-start | bytes 294920 | tf_op jit(solution)/shard_map/ppermute | solution.py:27
  262.5 33.2 %copy-start.7 = (bf16[64,4096]{1,0:T(8,128)(2,1)S(1)}, bf16[64,4096]{1,0:T(8,128)(2,1)}, u32[]{:S(2)}) copy-start(bf16[64,4096]{1,0:T(8,128)(2,1)} %param.14) | copy-start | bytes 1572868
  262.5 34.1 %copy-start.4 = (bf16[192,4096]{1,0:T(8,128)(2,1)S(1)}, bf16[192,4096]{1,0:T(8,128)(2,1)}, u32[]{:S(2)}) copy-start(bf16[192,4096]{1,0:T(8,128)(2,1)} %param.12) | copy-start | bytes 4718596
  265.7 32.6 %copy-start.6 = (bf16[192,2048]{1,0:T(8,128)(2,1)S(1)}, bf16[192,2048]{1,0:T(8,128)(2,1)}, u32[]{:S(2)}) copy-start(bf16[192,2048]{1,0:T(8,128)(2,1)} %param.13) | copy-start | bytes 2359300
  265.7 5.3 %collective-permute-start.8 = (f32[1,4,8,256]{3,2,0,1:T(8,128)S(1)}, f32[1,4,8,256]{3,2,0,1:T(8,128)S(1)}, u32[]{:S(2)}, u32[]{:S(2)}) collective-permute-start(f32[1,4,8,256]{3,2,0,1:T(8,128)S(1)} %maximum_bitcast_fusion), channel_id=1, source_target_pairs={{0,4},{4,0},{8,12},{12,8},{16,20},{20,16},{24,28},{28,24},{1,5},{5... | collective-permute-start | bytes 98312 | tf_op jit(solution)/shard_map/ppermute | solution.py:21
  271.0 4.8 %collective-permute-start.9 = (f32[2,4,8,256]{3,2,0,1:T(8,128)S(1)}, f32[2,4,8,256]{3,2,0,1:T(8,128)S(1)}, u32[]{:S(2)}, u32[]{:S(2)}) collective-permute-start(f32[2,4,8,256]{3,2,0,1:T(8,128)S(1)} %maximum_select_fusion.8), channel_id=1, source_target_pairs={{0,8},{4,12},{8,0},{12,4},{16,24},{20,28},{24,16},{28,20},{1,9},{5... | collective-permute-start | bytes 196616 | tf_op jit(solution)/shard_map/ppermute | solution.py:21
  (9 other events, 21.1 us)
where the time goes:
time: 300 us; the launch traced here: 299 us
  waiting for transfers between devices  114 us (38%)
  blocking collectives  83.7 us (28%)
  starting transfers between devices  46.2 us (15%)
  matrix products  29.9 us (10%)
  local copies, waits for them, and re-layouts  16 us (5%)
  other arithmetic  7.27 us (2%)
    ppermute x8, waiting for transfers between devices, from_partner(): return lax.ppermute(value, axis, pairs)  54.5 us
    all_gather x1, blocking collectives, body(): all_segs = lax.all_gather(segment_ids, 'seq', axis=0, tiled=True)  50.2 us
    all_to_all x1, waiting for transfers between devices, body(): lax.all_to_all(sent[1], 'seq', split_axis=0, concat_axis=1, tiled=True)  34.9 us
    all_to_all x1, waiting for transfers between devices, body(): lax.all_to_all(sent[2], 'seq', split_axis=0, concat_axis=1, tiled=True)  25 us
    ppermute x8, starting transfers between devices, from_partner(): return lax.ppermute(value, axis, pairs)  23.1 us
    pmax x1, blocking collectives, body(): head_max = lax.pmax(local_heads, 'seq')  19.1 us
    dot_general x4, matrix products, score_max(): jnp.einsum('qhd,kd->hqk', query_rope, key_rope, preferred_element_type=jn...  11.2 us
    all_gather x1, blocking collectives, body(): lax.all_gather(q_latent, 'head', axis=1, tiled=True)  8.59 us
  transfers between devices with their start and end apart: 13, of which 6 were waited for; matrix products, arithmetic and copies ran while one was open for 10% of the time, Pallas kernels for 0%

commit v1 on v0

--- a/solution.py
+++ b/solution.py
@@ -106,7 +106,12 @@
         .astype(jnp.bfloat16)
         .reshape(4 * rows, quarter, D_ROPE)
     )
-    all_segs = lax.all_gather(segment_ids, "seq", axis=0, tiled=True)
+    ring = [segment_ids]
+    for hop in range(7):
+        ring.append(lax.ppermute(ring[-1], "seq", [(dev, (dev + 1) % 8) for dev in range(8)]))
+    all_segs = jnp.roll(
+        jnp.concatenate(ring[::-1], axis=0), (lax.axis_index("seq") + 1) * ring[0].shape[0], axis=0
+    )
     padded_segs = jnp.concatenate([jnp.full((REACH * rows,), -1, jnp.int32), all_segs], 0)
     first = place // 4 * 4
     window = (REACH + 1) * rows

time: 300 us -> 311 us (1.037)
  waiting for transfers between devices: 114 us -> 167 us
  blocking collectives: 83.7 us -> 32.4 us
  starting transfers between devices: 46.2 us -> 53.6 us
    ppermute x0 -> x7, waiting for transfers between devices: none -> 85.8 us  [body(): lax.ppermute(ring[-1], 'seq', [(dev, (dev + 1) % 8) for dev in range(8)])]
    all_gather x1 -> x0, blocking collectives: 50.2 us -> none  [body(): all_segs = lax.all_gather(segment_ids, 'seq', axis=0, tiled=True)]
    all_to_all x1, waiting for transfers between devices: 34.9 us -> 0.01 us  [body(): lax.all_to_all(sent[1], 'seq', split_axis=0, concat_axis=1, tiled=True)]
    ppermute x0 -> x7, starting transfers between devices: none -> 13.1 us  [body(): lax.ppermute(ring[-1], 'seq', [(dev, (dev + 1) % 8) for dev in range(8)])]
    ppermute x8, starting transfers between devices: 23.1 us -> 13.3 us  [from_partner(): return lax.ppermute(value, axis, pairs)]
    ppermute x2, starting transfers between devices: 6.85 us -> 10.8 us  [shifted(): return lax.ppermute(block, axis, route)]
  transfers between devices with their start and end apart: 13 -> 20, of which waited for: 6 -> 11; matrix products, arithmetic and copies ran while one was open for 10% -> 12% of each run, Pallas kernels for 0% -> 0%
where the time goes in v1:
time: 311 us
  waiting for transfers between devices  167 us (54%)
  starting transfers between devices  53.6 us (17%)
  blocking collectives  32.4 us (10%)
  matrix products  29.9 us (10%)
  local copies, waits for them, and re-layouts  16.2 us (5%)
  other arithmetic  9.44 us (3%)
    ppermute x7, waiting for transfers between devices, body(): lax.ppermute(ring[-1], 'seq', [(dev, (dev + 1) % 8) for dev in range(8)])  85.8 us
    ppermute x8, waiting for transfers between devices, from_partner(): return lax.ppermute(value, axis, pairs)  56.6 us
    all_to_all x1, waiting for transfers between devices, body(): lax.all_to_all(sent[2], 'seq', split_axis=0, concat_axis=1, tiled=True)  25 us
    pmax x1, blocking collectives, body(): head_max = lax.pmax(local_heads, 'seq')  17.1 us
    ppermute x8, starting transfers between devices, from_partner(): return lax.ppermute(value, axis, pairs)  13.3 us
    ppermute x7, starting transfers between devices, body(): lax.ppermute(ring[-1], 'seq', [(dev, (dev + 1) % 8) for dev in range(8)])  13.1 us
    dot_general x4, matrix products, score_max(): jnp.einsum('qhd,kd->hqk', query_rope, key_rope, preferred_element_type=jn...  11.2 us
    ppermute x2, starting transfers between devices, shifted(): return lax.ppermute(block, axis, route)  10.8 us
  transfers between devices with their start and end apart: 20, of which 11 were waited for; matrix products, arithmetic and copies ran while one was open for 12% of the time, Pallas kernels for 0%

profile of v1, /device:TPU:0, one launch (start us, length us, event | category | flops | bytes accessed | tf_op | source)
XLA Modules:
  0.0 310.7 jit_solution(7416090284505098747)
XLA Ops:
  3.4 7.3 %all-to-all-start.1 = ((bf16[8,64,1024]{2,1,0:T(8,128)(2,1)}), bf16[8,64,1024]{2,1,0:T(8,128)(2,1)S(1)}, u32[]{:S(2)}, u32[]{:S(2)}) async-start(bf16[8,64,1024]{2,1,0:T(8,128)(2,1)} %bitcast.6), calls=%async_computation.1 | async-start | bytes 2097152 | tf_op jit(solution)/shard_map/all_to_all | solution.py:67
  11.5 25.0 %all-to-all-done.1 = bf16[8,64,1024]{2,1,0:T(8,128)(2,1)S(1)} async-done(((bf16[8,64,1024]{2,1,0:T(8,128)(2,1)}), bf16[8,64,1024]{2,1,0:T(8,128)(2,1)S(1)}, u32[]{:S(2)}, u32[]{:S(2)}) %all-to-all-start.1) | async-done | bytes 1048608 | tf_op jit(solution)/shard_map/all_to_all | solution.py:67
  37.9 4.4 %all-to-all-start.2 = ((bf16[8,192,512]{2,1,0:T(8,128)(2,1)}), bf16[8,192,512]{2,1,0:T(8,128)(2,1)}, u32[]{:S(2)}, u32[]{:S(2)}) async-start(bf16[8,192,512]{2,1,0:T(8,128)(2,1)} %bitcast.11), calls=%async_computation.2 | async-start | bytes 3145728 | tf_op jit(solution)/shard_map/all_to_all | solution.py:66
  45.7 6.3 %all_gather.7 = bf16[256,512]{1,0:T(8,128)(2,1)} all-gather(bf16[256,128]{1,0:T(8,128)(2,1)S(1)} %copy-done.15), channel_id=1, replica_groups=mesh['seq'=8,'head'=4] {'head'}, dimensions={1}, use_global_device_ids=true | all-gather | bytes 327680 | tf_op jit(solution)/shard_map/all_gather | solution.py:49
  52.5 9.0 %all_gather.6 = bf16[256,1536]{1,0:T(8,128)(2,1)} all-gather(bf16[256,384]{1,0:T(8,128)(2,1)S(1)} %copy-done.14), channel_id=1, replica_groups=mesh['seq'=8,'head'=4] {'head'}, dimensions={1}, use_global_device_ids=true | all-gather | bytes 983040 | tf_op jit(solution)/shard_map/all_gather | solution.py:48
  63.1 9.2 %collective-permute-done = s32[256]{0:T(256)S(1)} collective-permute-done((s32[256]{0:T(256)S(1)}, s32[256]{0:T(256)S(1)}, u32[]{:S(2)}, u32[]{:S(2)}) %collective-permute-start) | collective-permute-done | bytes 1056 | tf_op jit(solution)/shard_map/ppermute | solution.py:111
  74.0 9.5 %collective-permute-done.1 = s32[256]{0:T(256)S(1)} collective-permute-done((s32[256]{0:T(256)S(1)}, s32[256]{0:T(256)S(1)}, u32[]{:S(2)}, u32[]{:S(2)}) %collective-permute-start.1) | collective-permute-done | bytes 1056 | tf_op jit(solution)/shard_map/ppermute | solution.py:111
  88.1 4.7 %all-to-all-start = ((bf16[8,192,1024]{2,1,0:T(8,128)(2,1)}), bf16[8,192,1024]{2,1,0:T(8,128)(2,1)}, u32[]{:S(2)}, u32[]{:S(2)}) async-start(bf16[8,192,1024]{2,1,0:T(8,128)(2,1)} %bitcast.2), calls=%async_computation | async-start | bytes 6291456 | tf_op jit(solution)/shard_map/all_to_all | solution.py:65
  94.9 53.3 %collective-permute-done.3 = s32[256]{0:T(256)S(1)} collective-permute-done((s32[256]{0:T(256)S(1)}, s32[256]{0:T(256)S(1)}, u32[]{:S(2)}, u32[]{:S(2)}) %collective-permute-start.3) | collective-permute-done | bytes 1056 | tf_op jit(solution)/shard_map/ppermute | solution.py:111
  148.2 6.3 %collective-permute-done.4 = s32[256]{0:T(256)S(1)} collective-permute-done((s32[256]{0:T(256)S(1)}, s32[256]{0:T(256)S(1)}, u32[]{:S(2)}, u32[]{:S(2)}) %collective-permute-start.4) | collective-permute-done | bytes 1056 | tf_op jit(solution)/shard_map/ppermute | solution.py:111
  154.5 6.3 %collective-permute-done.5 = s32[256]{0:T(256)S(1)} collective-permute-done((s32[256]{0:T(256)S(1)}, s32[256]{0:T(256)S(1)}, u32[]{:S(2)}, u32[]{:S(2)}) %collective-permute-start.5) | collective-permute-done | bytes 1056 | tf_op jit(solution)/shard_map/ppermute | solution.py:111
  160.7 6.6 %collective-permute-start.6 = (s32[256]{0:T(256)S(1)}, s32[256]{0:T(256)S(1)}, u32[]{:S(2)}, u32[]{:S(2)}) collective-permute-start(s32[256]{0:T(256)S(1)} %collective-permute-done.5), channel_id=1, source_target_pairs={{0,4},{4,8},{8,12},{12,16},{16,20},{20,24},{24,28},{28,0},{1,5},{5... | collective-permute-start | bytes 3080 | tf_op jit(solution)/shard_map/ppermute | solution.py:111
  170.2 5.1 %collective-permute-start.10 = (bf16[512,512]{1,0:T(8,128)(2,1)S(1)}, bf16[512,512]{1,0:T(8,128)(2,1)S(1)}, u32[]{:S(2)}, u32[]{:S(2)}) collective-permute-start(bf16[512,512]{1,0:T(8,128)(2,1)S(1)} %maximum_select_fusion.5), channel_id=1, source_target_pairs={{0,8},{4,12},{8,0},{12,4},{16,24},{20,28},{24,16},{28,20},{1,9},{5... | collective-permute-start | bytes 1572872 | tf_op jit(solution)/shard_map/ppermute | solution.py:21
  176.1 8.1 %collective-permute-done.10 = bf16[512,512]{1,0:T(8,128)(2,1)S(1)} collective-permute-done((bf16[512,512]{1,0:T(8,128)(2,1)S(1)}, bf16[512,512]{1,0:T(8,128)(2,1)S(1)}, u32[]{:S(2)}, u32[]{:S(2)}) %collective-permute-start.10) | collective-permute-done | bytes 524320 | tf_op jit(solution)/shard_map/ppermute | solution.py:21
  184.7 7.6 %collective-permute-start.11 = (bf16[768,512]{1,0:T(8,128)(2,1)S(1)}, bf16[768,512]{1,0:T(8,128)(2,1)S(1)}, u32[]{:S(2)}, u32[]{:S(2)}) collective-permute-start(bf16[768,512]{1,0:T(8,128)(2,1)S(1)} %slice.117), channel_id=1, source_target_pairs={{0,16},{4,20},{8,24},{12,28},{1,17},{5,21},{9,25},{13,29},{2,18},{... | collective-permute-start | bytes 2359304 | tf_op jit(solution)/shard_map/ppermute | solution.py:27
  197.5 43.0 %collective-permute-done.13 = bf16[512,64]{0,1:T(8,128)(2,1)S(1)} collective-permute-done((bf16[512,64]{0,1:T(8,128)(2,1)S(1)}, bf16[512,64]{0,1:T(8,128)(2,1)S(1)}, u32[]{:S(2)}, u32[]{:S(2)}) %collective-permute-start.13) | collective-permute-done | bytes 65568 | tf_op jit(solution)/shard_map/ppermute | solution.py:21
  241.2 3.2 %collective-permute-start.14 = (bf16[768,64]{0,1:T(8,128)(2,1)}, bf16[768,64]{0,1:T(8,128)(2,1)}, u32[]{:S(2)}, u32[]{:S(2)}) collective-permute-start(bf16[768,64]{0,1:T(8,128)(2,1)} %slice.119), channel_id=1, source_target_pairs={{0,16},{4,20},{8,24},{12,28},{1,17},{5,21},{9,25},{13,29},{2,18},{... | collective-permute-start | bytes 294920 | tf_op jit(solution)/shard_map/ppermute | solution.py:27
  246.6 2.9 fusion.37
  249.6 3.9 %multiply_convert_fusion.3 = bf16[1024,512]{0,1:T(8,128)(2,1)S(1)} fusion(bf16[1536,512]{1,0:T(8,128)(2,1)} %bitcast.12, bf16[512,1536]{1,0:T(8,128)(2,1)S(1)} %maximum_select_fusion.1, bf16[512,1536]{1,0:T(8,128)(2,1)S(1)} %collective-permute-done.8, pred[]{:T(512)S(6)} %eq.85), kind=kOutput, calls=%fused_computation.20 | convolution fusion | flops 1625817088 | bytes 5767169 | tf_op jit(solution)/shard_map/dot_general | solution.py:105
  254.4 7.2 %multiply_convert_fusion.1 = bf16[1024,1024]{0,1:T(8,128)(2,1)S(1)} fusion(bf16[1536,1024]{1,0:T(8,128)(2,1)} %bitcast.3, bf16[512,1536]{1,0:T(8,128)(2,1)} %copy-done.8, bf16[512,1536]{1,0:T(8,128)(2,1)} %copy-done.19, pred[]{:T(512)S(6)} %eq.85), kind=kOutput, calls=%fused_computation.17 | convolution fusion | flops 3237478400 | bytes 8388609 | tf_op jit(solution)/shard_map/dot_general | solution.py:100
  271.4 3.0 fusion.11
  277.4 3.1 %fusion.8 = f32[8,256]{1,0:T(8,128)S(1)} fusion(f32[8,256,1024]{2,1,0:T(8,128)S(1)} %fusion.42, pred[256,1024]{1,0:T(8,128)(4,1)S(1)} %get-tuple-element.30, bf16[256,8,64]{0,2,1:T(8,128)(2,1)S(1)} %bitcast.105, bf16[1024,64]{0,1:T(8,128)(2,1)S(1)} %maximum_select_fusion.6, bf16[768,64]{0,1:T(8,128)(2,1)} %collective-permute-done.14), kind=kOutput, calls=%fused_computation.11 | convolution fusion | flops 277084160 | bytes 9150464 | tf_op jit(solution)/shard_map/qhd,kd->hqk/dot_general | solution.py:32
  280.6 3.9 %collective-permute-done.15 = f32[1,4,8,256]{3,2,0,1:T(8,128)S(1)} collective-permute-done((f32[1,4,8,256]{3,2,0,1:T(8,128)S(1)}, f32[1,4,8,256]{3,2,0,1:T(8,128)S(1)}, u32[]{:S(2)}, u32[]{:S(2)}) %collective-permute-start.15) | collective-permute-done | bytes 32800 | tf_op jit(solution)/shard_map/ppermute | solution.py:21
  290.0 17.1 %pmax.7 = f32[32]{0:T(128)S(1)} all-reduce(f32[32]{0:T(128)S(1)} %reduce_max.52), channel_id=1, replica_groups=mesh['seq'=8,'head'=4] {'seq'}, use_global_device_ids=true, to_apply=%region_5.6 | all-reduce | flops 32 | bytes 256 | tf_op jit(solution)/shard_map/pmax | solution.py:148
  (135 shorter events, 52.8 us)
Async XLA Ops:
  3.4 33.0 %all-to-all-start.1 = ((bf16[8,64,1024]{2,1,0:T(8,128)(2,1)}), bf16[8,64,1024]{2,1,0:T(8,128)(2,1)S(1)}, u32[]{:S(2)}, u32[]{:S(2)}) async-start(bf16[8,64,1024]{2,1,0:T(8,128)(2,1)} %bitcast.6), calls=%async_computation.1 | async-start | bytes 2097152 | tf_op jit(solution)/shard_map/all_to_all | solution.py:67
  11.5 34.2 %copy-start.15 = (bf16[256,128]{1,0:T(8,128)(2,1)S(1)}, bf16[256,128]{1,0:T(8,128)(2,1)}, u32[]{:S(2)}) copy-start(bf16[256,128]{1,0:T(8,128)(2,1)} %param.9) | copy-start | bytes 196612
  11.5 60.8 %copy-start.3 = (bf16[192,4096]{1,0:T(8,128)(2,1)S(1)}, bf16[192,4096]{1,0:T(8,128)(2,1)}, u32[]{:S(2)}) copy-start(bf16[192,4096]{1,0:T(8,128)(2,1)} %param.12) | copy-start | bytes 4718596
  37.9 48.1 %all-to-all-start.2 = ((bf16[8,192,512]{2,1,0:T(8,128)(2,1)}), bf16[8,192,512]{2,1,0:T(8,128)(2,1)}, u32[]{:S(2)}, u32[]{:S(2)}) async-start(bf16[8,192,512]{2,1,0:T(8,128)(2,1)} %bitcast.11), calls=%async_computation.2 | async-start | bytes 3145728 | tf_op jit(solution)/shard_map/all_to_all | solution.py:66
  42.3 30.0 %collective-permute-start = (s32[256]{0:T(256)S(1)}, s32[256]{0:T(256)S(1)}, u32[]{:S(2)}, u32[]{:S(2)}) collective-permute-start(s32[256]{0:T(256)S(1)} %copy-done.17), channel_id=1, source_target_pairs={{0,4},{4,8},{8,12},{12,16},{16,20},{20,24},{24,28},{28,0},{1,5},{5... | collective-permute-start | bytes 3080 | tf_op jit(solution)/shard_map/ppermute | solution.py:111
  44.2 151.1 %collective-permute-start.12 = (bf16[256,64]{0,1:T(8,128)(2,1)S(1)}, bf16[256,64]{0,1:T(8,128)(2,1)S(1)}, u32[]{:S(2)}, u32[]{:S(2)}) collective-permute-start(bf16[256,64]{0,1:T(8,128)(2,1)S(1)} %copy-done.16), channel_id=1, source_target_pairs={{0,4},{4,0},{8,12},{12,8},{16,20},{20,16},{24,28},{28,24},{1,5},{5... | collective-permute-start | bytes 98312 | tf_op jit(solution)/shard_map/ppermute | solution.py:21
  51.9 116.9 %collective-permute-start.9 = (bf16[256,512]{1,0:T(8,128)(2,1)}, bf16[256,512]{1,0:T(8,128)(2,1)}, u32[]{:S(2)}, u32[]{:S(2)}) collective-permute-start(bf16[256,512]{1,0:T(8,128)(2,1)} %all_gather.7), channel_id=1, source_target_pairs={{0,4},{4,0},{8,12},{12,8},{16,20},{20,16},{24,28},{28,24},{1,5},{5... | collective-permute-start | bytes 786440 | tf_op jit(solution)/shard_map/ppermute | solution.py:21
  61.5 130.8 %collective-permute-start.7 = (bf16[256,1536]{1,0:T(8,128)(2,1)}, bf16[256,1536]{1,0:T(8,128)(2,1)}, u32[]{:S(2)}, u32[]{:S(2)}) collective-permute-start(bf16[256,1536]{1,0:T(8,128)(2,1)} %all_gather.6), channel_id=1, source_target_pairs={{0,4},{4,0},{8,12},{12,8},{16,20},{20,16},{24,28},{28,24},{1,5},{5... | collective-permute-start | bytes 2359304 | tf_op jit(solution)/shard_map/ppermute | solution.py:21
  72.3 11.2 %collective-permute-start.1 = (s32[256]{0:T(256)S(1)}, s32[256]{0:T(256)S(1)}, u32[]{:S(2)}, u32[]{:S(2)}) collective-permute-start(s32[256]{0:T(256)S(1)} %collective-permute-done), channel_id=1, source_target_pairs={{0,4},{4,8},{8,12},{12,16},{16,20},{20,24},{24,28},{28,0},{1,5},{5... | collective-permute-start | bytes 3080 | tf_op jit(solution)/shard_map/ppermute | solution.py:111
  83.5 9.4 %collective-permute-start.2 = (s32[256]{0:T(256)S(1)}, s32[256]{0:T(256)S(1)}, u32[]{:S(2)}, u32[]{:S(2)}) collective-permute-start(s32[256]{0:T(256)S(1)} %collective-permute-done.1), channel_id=1, source_target_pairs={{0,4},{4,8},{8,12},{12,16},{16,20},{20,24},{24,28},{28,0},{1,5},{5... | collective-permute-start | bytes 3080 | tf_op jit(solution)/shard_map/ppermute | solution.py:111
  88.1 166.3 %all-to-all-start = ((bf16[8,192,1024]{2,1,0:T(8,128)(2,1)}), bf16[8,192,1024]{2,1,0:T(8,128)(2,1)}, u32[]{:S(2)}, u32[]{:S(2)}) async-start(bf16[8,192,1024]{2,1,0:T(8,128)(2,1)} %bitcast.2), calls=%async_computation | async-start | bytes 6291456 | tf_op jit(solution)/shard_map/all_to_all | solution.py:65
  92.9 55.3 %collective-permute-start.3 = (s32[256]{0:T(256)S(1)}, s32[256]{0:T(256)S(1)}, u32[]{:S(2)}, u32[]{:S(2)}) collective-permute-start(s32[256]{0:T(256)S(1)} %collective-permute-done.2), channel_id=1, source_target_pairs={{0,4},{4,8},{8,12},{12,16},{16,20},{20,24},{24,28},{28,0},{1,5},{5... | collective-permute-start | bytes 3080 | tf_op jit(solution)/shard_map/ppermute | solution.py:111
  148.2 6.3 %collective-permute-start.4 = (s32[256]{0:T(256)S(1)}, s32[256]{0:T(256)S(1)}, u32[]{:S(2)}, u32[]{:S(2)}) collective-permute-start(s32[256]{0:T(256)S(1)} %collective-permute-done.3), channel_id=1, source_target_pairs={{0,4},{4,8},{8,12},{12,16},{16,20},{20,24},{24,28},{28,0},{1,5},{5... | collective-permute-start | bytes 3080 | tf_op jit(solution)/shard_map/ppermute | solution.py:111
  154.5 6.3 %collective-permute-start.5 = (s32[256]{0:T(256)S(1)}, s32[256]{0:T(256)S(1)}, u32[]{:S(2)}, u32[]{:S(2)}) collective-permute-start(s32[256]{0:T(256)S(1)} %collective-permute-done.4), channel_id=1, source_target_pairs={{0,4},{4,8},{8,12},{12,16},{16,20},{20,24},{24,28},{28,0},{1,5},{5... | collective-permute-start | bytes 3080 | tf_op jit(solution)/shard_map/ppermute | solution.py:111
  160.7 7.9 %collective-permute-start.6 = (s32[256]{0:T(256)S(1)}, s32[256]{0:T(256)S(1)}, u32[]{:S(2)}, u32[]{:S(2)}) collective-permute-start(s32[256]{0:T(256)S(1)} %collective-permute-done.5), channel_id=1, source_target_pairs={{0,4},{4,8},{8,12},{12,16},{16,20},{20,24},{24,28},{28,0},{1,5},{5... | collective-permute-start | bytes 3080 | tf_op jit(solution)/shard_map/ppermute | solution.py:111
  170.2 14.0 %collective-permute-start.10 = (bf16[512,512]{1,0:T(8,128)(2,1)S(1)}, bf16[512,512]{1,0:T(8,128)(2,1)S(1)}, u32[]{:S(2)}, u32[]{:S(2)}) collective-permute-start(bf16[512,512]{1,0:T(8,128)(2,1)S(1)} %maximum_select_fusion.5), channel_id=1, source_target_pairs={{0,8},{4,12},{8,0},{12,4},{16,24},{20,28},{24,16},{28,20},{1,9},{5... | collective-permute-start | bytes 1572872 | tf_op jit(solution)/shard_map/ppermute | solution.py:21
  184.7 59.7 %copy-start.10 = (bf16[8,64,1024]{2,1,0:T(8,128)(2,1)S(1)}, bf16[8,64,1024]{2,1,0:T(8,128)(2,1)}, u32[]{:S(2)}) copy-start(bf16[8,64,1024]{2,1,0:T(8,128)(2,1)} %copy-done.9) | copy-start | bytes 3145732
  184.7 59.7 %collective-permute-start.11 = (bf16[768,512]{1,0:T(8,128)(2,1)S(1)}, bf16[768,512]{1,0:T(8,128)(2,1)S(1)}, u32[]{:S(2)}, u32[]{:S(2)}) collective-permute-start(bf16[768,512]{1,0:T(8,128)(2,1)S(1)} %slice.117), channel_id=1, source_target_pairs={{0,16},{4,20},{8,24},{12,28},{1,17},{5,21},{9,25},{13,29},{2,18},{... | collective-permute-start | bytes 2359304 | tf_op jit(solution)/shard_map/ppermute | solution.py:27
  194.6 54.9 %copy-start.8 = (bf16[512,1536]{1,0:T(8,128)(2,1)}, bf16[512,1536]{1,0:T(8,128)(2,1)S(1)}, u32[]{:S(2)}) copy-start(bf16[512,1536]{1,0:T(8,128)(2,1)S(1)} %maximum_select_fusion.1) | copy-start | bytes 4718596
  194.6 54.9 %collective-permute-start.8 = (bf16[512,1536]{1,0:T(8,128)(2,1)S(1)}, bf16[512,1536]{1,0:T(8,128)(2,1)S(1)}, u32[]{:S(2)}, u32[]{:S(2)}) collective-permute-start(bf16[512,1536]{1,0:T(8,128)(2,1)S(1)} %maximum_select_fusion.1), channel_id=1, source_target_pairs={{0,8},{4,12},{8,0},{12,4},{16,24},{20,28},{24,16},{28,20},{1,9},{5... | collective-permute-start | bytes 4718600 | tf_op jit(solution)/shard_map/ppermute | solution.py:21
  195.3 45.2 %collective-permute-start.13 = (bf16[512,64]{0,1:T(8,128)(2,1)S(1)}, bf16[512,64]{0,1:T(8,128)(2,1)S(1)}, u32[]{:S(2)}, u32[]{:S(2)}) collective-permute-start(bf16[512,64]{0,1:T(8,128)(2,1)S(1)} %maximum_select_fusion.7), channel_id=1, source_target_pairs={{0,8},{4,12},{8,0},{12,4},{16,24},{20,28},{24,16},{28,20},{1,9},{5... | collective-permute-start | bytes 196616 | tf_op jit(solution)/shard_map/ppermute | solution.py:21
  241.2 30.2 %collective-permute-start.14 = (bf16[768,64]{0,1:T(8,128)(2,1)}, bf16[768,64]{0,1:T(8,128)(2,1)}, u32[]{:S(2)}, u32[]{:S(2)}) collective-permute-start(bf16[768,64]{0,1:T(8,128)(2,1)} %slice.119), channel_id=1, source_target_pairs={{0,16},{4,20},{8,24},{12,28},{1,17},{5,21},{9,25},{13,29},{2,18},{... | collective-permute-start | bytes 294920 | tf_op jit(solution)/shard_map/ppermute | solution.py:27
  280.5 4.0 %collective-permute-start.15 = (f32[1,4,8,256]{3,2,0,1:T(8,128)S(1)}, f32[1,4,8,256]{3,2,0,1:T(8,128)S(1)}, u32[]{:S(2)}, u32[]{:S(2)}) collective-permute-start(f32[1,4,8,256]{3,2,0,1:T(8,128)S(1)} %maximum_bitcast_fusion), channel_id=1, source_target_pairs={{0,4},{4,0},{8,12},{12,8},{16,20},{20,16},{24,28},{28,24},{1,5},{5... | collective-permute-start | bytes 98312 | tf_op jit(solution)/shard_map/ppermute | solution.py:21
  284.5 4.8 %collective-permute-start.16 = (f32[2,4,8,256]{3,2,0,1:T(8,128)S(1)}, f32[2,4,8,256]{3,2,0,1:T(8,128)S(1)}, u32[]{:S(2)}, u32[]{:S(2)}) collective-permute-start(f32[2,4,8,256]{3,2,0,1:T(8,128)S(1)} %maximum_select_fusion.8), channel_id=1, source_target_pairs={{0,8},{4,12},{8,0},{12,4},{16,24},{20,28},{24,16},{28,20},{1,9},{5... | collective-permute-start | bytes 196616 | tf_op jit(solution)/shard_map/ppermute | solution.py:21
  (16 other events, 221.4 us)
